TPU v7x, 256 devices: a 8x8x2 block of a 8x8x16 slice. The times are simulated.
256 devices in a mesh: grp: 2 (over z), row: 64 (over y, x), col: 2 (over core).
Axes of the slice: x: 8, y: 8, z: 2, core: 2. Of those that a mesh axis runs over, the one named last changes fastest.
The devices are a block of a 8x8x16 slice.
Arguments:
- factors: bfloat16 [2, 12288, 6144], P(None, ('grp', 'row'), 'col'), parts along dimension 1, may hold values from -6 to 6
- orbitals: bfloat16 [12288, 1024], P(('grp', 'row'), 'col'), parts along dimension 0, may hold values from -0.02734375 to 0.02734375
- field_term: bfloat16 [12288, 6144], P(('grp', 'row'), 'col'), parts along dimension 0, may hold values from -1.5 to 1.5
Outputs:
- fock_matrix: bfloat16 [12288, 6144], P(('grp', 'row'), 'col'), parts along dimension 0
There are 2 independent parts, one for each index of `grp`. A program takes and returns all parts, laid end to end along the dimension named above; each array names one. Nothing has to cross between parts.
All inputs are finite; a program needn't handle non-finite values.
Results may differ from a plain program's by a relative error of at most 0.02.
Values may be sent and summed in bfloat16 or wider, within the bound.
A program may use at most 64 MiB of HBM per device.

v0:
```python
import functools
import jax
import jax.numpy as jnp
from jax import lax
from jax.sharding import Mesh
from jax.sharding import PartitionSpec as P

ROW = ("row_0", "row_1")
ROW_COL = ("row_0", "row_1", "col")
GRP_ROW = ("grp", "row_0", "row_1")


def copy_for_each(value, axis):
    size = lax.axis_size(axis)
    return lax.all_to_all(
        jnp.broadcast_to(value[None], (size, *value.shape)), axis, 0, 0, tiled=True
    )


def joined_along(tiles, dim):
    tiles = jnp.moveaxis(tiles, 0, dim)
    dims = tiles.shape
    return tiles.reshape(*dims[:dim], dims[dim] * dims[dim + 1], *dims[dim + 2 :])


def collect(value, axis, dim):
    tiles = copy_for_each(value, axis)
    return joined_along(tiles, dim)


def split_up(value, dim, size):
    before, after = (value.shape[:dim], value.shape[dim + 1 :])
    return jnp.moveaxis(value.reshape(*before, size, -1, *after), dim, 0)


def sum_at_owner(value, axis, dim):
    tiles = split_up(value, dim, lax.axis_size(axis))
    arrived = lax.all_to_all(tiles, axis, split_axis=0, concat_axis=0, tiled=True)
    return arrived.astype(jnp.float32).sum(axis=0)


def by_axis(value, axes):
    return functools.reduce(lax.psum, axes, value)


def shards(factors, orbitals, field_term):
    aux_count = factors.shape[0]
    all_orbitals = lax.all_gather(orbitals, ROW, axis=0, tiled=True)
    orbit_wide = orbitals.astype(jnp.float32)
    exchange = None
    gammas = []
    for aux in range(aux_count):
        half_local = jnp.dot(
            collect(factors[aux], "col", 1), all_orbitals, preferred_element_type=jnp.float32
        ).astype(jnp.bfloat16)
        local_fit = jnp.sum(half_local.astype(jnp.float32) * orbit_wide)
        gammas.append(local_fit)
        term = lax.dot_general(
            half_local,
            lax.all_gather(half_local, ROW, axis=0, tiled=True),
            (((1,), (1,)), ((), ())),
            preferred_element_type=jnp.float32,
        )
        reduced = sum_at_owner(term.astype(jnp.bfloat16), "col", 1)
        exchange = reduced if exchange is None else exchange + reduced
    fitted = by_axis(jnp.stack(gammas), ROW_COL)
    gammas = [fitted[aux] for aux in range(aux_count)]
    coulomb = jnp.zeros(field_term.shape, jnp.float32)
    for aux in range(aux_count):
        coulomb = coulomb + gammas[aux] * factors[aux].astype(jnp.float32)
    fock_matrix = field_term.astype(jnp.float32) + coulomb - 0.25 * exchange
    return fock_matrix.astype(jnp.bfloat16)


def solution(mesh):
    finer = Mesh(
        mesh.devices.reshape(mesh.shape["grp"], 8, 8, mesh.shape["col"]),
        ("grp", "row_0", "row_1", "col"),
    )
    return jax.shard_map(
        shards,
        mesh=finer,
        in_specs=(P(None, GRP_ROW, "col"), P(GRP_ROW, "col"), P(GRP_ROW, "col")),
        out_specs=P(GRP_ROW, "col"),
        check_vma=False,
    )
```

profile of v0, /device:TPU:513, one launch (start us, length us, event | category | flops | bytes accessed | tf_op | source)
XLA Modules:
  0.0 318.9 jit_solution(6659823777059124831)
XLA Ops:
  6.6 0.7 all-gather.4.cloned.1.call-update
  7.3 1.3 slice_bitcast_fusion
  8.6 0.1 broadcast_in_dim.17
  8.8 24.7 %all_to_all.20 = bf16[2,96,3072]{2,1,0:T(8,128)(2,1)S(1)} all-to-all(bf16[2,96,3072]{2,1,0:T(8,128)(2,1)S(1)} %broadcast_in_dim.17), channel_id=1, replica_groups=mesh['grp'=2,'row_0'=8,'row_1'=8,'col'=2] {'col'}, dimensions={0} | all-to-all | bytes 2359296 | tf_op jit(solution)/shard_map/all_to_all | solution.py:15
  33.5 1.2 broadcast_in_dim.15
  34.7 4.0 %all-to-all-start = ((bf16[2,96,3072]{2,1,0:T(8,128)(2,1)}), bf16[2,96,3072]{2,1,0:T(8,128)(2,1)S(1)}, u32[]{:S(2)}, u32[]{:S(2)}) async-start(bf16[2,96,3072]{2,1,0:T(8,128)(2,1)} %broadcast_in_dim.15), calls=%async_computation | async-start | bytes 2359296 | tf_op jit(solution)/shard_map/all_to_all | solution.py:15
  38.7 0.1 copy.11
  38.8 1.7 all-to-all-done
  40.5 0.1 copy.10
  40.6 73.8 %all-gather.4.cloned.1.call-done = bf16[6144,512]{1,0:T(8,128)(2,1)} async-done(((bf16[96,512]{1,0:T(8,128)(2,1)}), bf16[6144,512]{1,0:T(8,128)(2,1)}) %all-gather.4.cloned.1.call-update) | async-done | bytes 6291472 | tf_op jit(solution)/shard_map/all_gather | solution.py:48
  114.4 3.9 %convolution_convert_fusion.2 = bf16[96,512]{1,0:T(8,128)(2,1)S(1)} fusion(bf16[96,6144]{1,0:T(8,128)(2,1)S(1)} %bitcast.45, bf16[6144,512]{1,0:T(8,128)(2,1)} %all-gather.4.cloned.1.call-done), kind=kOutput, calls=%fused_computation.7 | convolution fusion | flops 604028928 | bytes 7569408 | tf_op jit(solution)/shard_map/dot_general | solution.py:53
  118.3 5.2 %fusion = (f32[]{:T(128)}, f32[]{:T(128)}, bf16[96,512]{1,0:T(8,128)(2,1)}) fusion(bf16[96,512]{1,0:T(8,128)(2,1)S(1)} %copy-done.4, bf16[96,512]{1,0:T(8,128)(2,1)S(1)} %convolution_convert_fusion.2, bf16[96,6144]{1,0:T(8,128)(2,1)S(1)} %bitcast.42, bf16[6144,512]{1,0:T(8,128)(2,1)} %all-gather.4.cloned.1.call-done), kind=kOutput, calls=%fused_computation.13 | convolution fusion | flops 604372992 | bytes 7766024 | tf_op jit(solution)/shard_map/dot_general | solution.py:53
  123.6 0.1 all-gather.8.cloned.1.call-start
  123.7 0.7 all-gather.8.cloned.1.call-update
  124.4 1.2 pad_maximum_fusion
  125.6 12.1 %psum.21 = f32[2]{0:T(128)S(1)} all-reduce(f32[2]{0:T(128)S(1)} %pad_maximum_fusion), channel_id=1, replica_groups=mesh['grp'=2,'row_0'=8,'row_1'=8,'col'=2] {'row_0'}, use_global_device_ids=true, to_apply=%region_2.0 | all-reduce | flops 2 | bytes 16 | tf_op jit(solution)/shard_map/psum | solution.py:43
  137.7 12.8 %psum.22 = f32[2]{0:T(128)S(1)} all-reduce(f32[2]{0:T(128)S(1)} %psum.21), channel_id=1, replica_groups=mesh['grp'=2,'row_0'=8,'row_1'=8,'col'=2] {'row_1'}, use_global_device_ids=true, to_apply=%region_3.0 | all-reduce | flops 2 | bytes 16 | tf_op jit(solution)/shard_map/psum | solution.py:43
  150.5 11.3 %psum.23 = f32[2]{0:T(128)S(1)} all-reduce(f32[2]{0:T(128)S(1)} %psum.22), channel_id=1, replica_groups=mesh['grp'=2,'row_0'=8,'row_1'=8,'col'=2] {'col'}, use_global_device_ids=true, to_apply=%region_4.0 | all-reduce | flops 2 | bytes 16 | tf_op jit(solution)/shard_map/psum | solution.py:43
  161.8 0.6 fusion.2
  162.4 45.8 %all-gather.6.cloned.1.call-done = bf16[6144,512]{1,0:T(8,128)(2,1)} async-done(((bf16[96,512]{1,0:T(8,128)(2,1)}), bf16[6144,512]{1,0:T(8,128)(2,1)}) %all-gather.6.cloned.1.call-update) | async-done | bytes 6291472 | tf_op jit(solution)/shard_map/all_gather | solution.py:60
  208.2 4.8 %convolution_convert_fusion.1 = bf16[96,6144]{1,0:T(8,128)(2,1)S(1)} fusion(bf16[96,512]{1,0:T(8,128)(2,1)} %get-tuple-element.11, bf16[6144,512]{1,0:T(8,128)(2,1)} %all-gather.6.cloned.1.call-done), kind=kOutput, calls=%fused_computation.1 | convolution fusion | flops 604569600 | bytes 7569408 | tf_op jit(solution)/shard_map/dot_general | solution.py:58
  213.1 1.1 copy.15
  214.2 6.1 %all-to-all-start.2 = ((bf16[2,96,3072]{2,1,0:T(8,128)(2,1)}), bf16[2,96,3072]{2,1,0:T(8,128)(2,1)S(1)}, u32[]{:S(2)}, u32[]{:S(2)}) async-start(bf16[2,96,3072]{2,1,0:T(8,128)(2,1)} %bitcast.39), calls=%async_computation.2 | async-start | bytes 2359296 | tf_op jit(solution)/shard_map/all_to_all | solution.py:38
  220.2 74.9 %all-gather.8.cloned.1.call-done = bf16[6144,512]{1,0:T(8,128)(2,1)} async-done(((bf16[96,512]{1,0:T(8,128)(2,1)}), bf16[6144,512]{1,0:T(8,128)(2,1)}) %all-gather.8.cloned.1.call-update) | async-done | bytes 6291472 | tf_op jit(solution)/shard_map/all_gather | solution.py:60
  295.2 4.8 %convolution_convert_fusion = bf16[96,6144]{1,0:T(8,128)(2,1)S(1)} fusion(bf16[96,512]{1,0:T(8,128)(2,1)S(1)} %copy-done.2, bf16[6144,512]{1,0:T(8,128)(2,1)} %all-gather.8.cloned.1.call-done), kind=kOutput, calls=%fused_computation | convolution fusion | flops 604569600 | bytes 7569408 | tf_op jit(solution)/shard_map/dot_general | solution.py:58
  300.0 1.1 copy.14
  301.1 5.9 %all-to-all-start.3 = ((bf16[2,96,3072]{2,1,0:T(8,128)(2,1)}), bf16[2,96,3072]{2,1,0:T(8,128)(2,1)S(1)}, u32[]{:S(2)}, u32[]{:S(2)}) async-start(bf16[2,96,3072]{2,1,0:T(8,128)(2,1)} %bitcast.37), calls=%async_computation.3 | async-start | bytes 2359296 | tf_op jit(solution)/shard_map/all_to_all | solution.py:38
  307.0 0.2 convert_reduce_fusion.1
  307.2 1.6 all-to-all-done.3
  308.8 0.2 convert_reduce_fusion
  309.1 0.8 copy-done.3
  309.9 2.4 subtract_convert_fusion
  (13 shorter events, 0.1 us)
Async XLA Ops:
  6.5 107.8 %all-gather.4.cloned.1.call-start = ((), (), s32[]{:S(2)}) async-start(), calls=%async_computation.4 | async-start | bytes 6389760 | tf_op jit(solution)/shard_map/all_gather | solution.py:48
  34.7 5.8 %all-to-all-start = ((bf16[2,96,3072]{2,1,0:T(8,128)(2,1)}), bf16[2,96,3072]{2,1,0:T(8,128)(2,1)S(1)}, u32[]{:S(2)}, u32[]{:S(2)}) async-start(bf16[2,96,3072]{2,1,0:T(8,128)(2,1)} %broadcast_in_dim.15), calls=%async_computation | async-start | bytes 2359296 | tf_op jit(solution)/shard_map/all_to_all | solution.py:15
  38.7 169.6 %all-gather.6.cloned.1.call-start = ((), (), s32[]{:S(2)}) async-start(), calls=%async_computation.5 | async-start | bytes 6389760 | tf_op jit(solution)/shard_map/all_gather | solution.py:60
  114.3 4.0 %copy-start.4 = (bf16[96,512]{1,0:T(8,128)(2,1)S(1)}, bf16[96,512]{1,0:T(8,128)(2,1)}, u32[]{:S(2)}) copy-start(bf16[96,512]{1,0:T(8,128)(2,1)} %param.4) | copy-start | bytes 294916
  118.3 5.2 %copy-start.1 = (bf16[96,512]{1,0:T(8,128)(2,1)}, bf16[96,512]{1,0:T(8,128)(2,1)S(1)}, u32[]{:S(2)}) copy-start(bf16[96,512]{1,0:T(8,128)(2,1)S(1)} %convolution_convert_fusion.2) | copy-start | bytes 294916
  123.6 171.6 %all-gather.8.cloned.1.call-start = ((), (), s32[]{:S(2)}) async-start(), calls=%async_computation.6 | async-start | bytes 6389760 | tf_op jit(solution)/shard_map/all_gather | solution.py:60
  214.2 81.0 %copy-start.2 = (bf16[96,512]{1,0:T(8,128)(2,1)S(1)}, bf16[96,512]{1,0:T(8,128)(2,1)}, u32[]{:S(2)}) copy-start(bf16[96,512]{1,0:T(8,128)(2,1)} %copy-done.1) | copy-start | bytes 294916
  214.2 86.9 %all-to-all-start.2 = ((bf16[2,96,3072]{2,1,0:T(8,128)(2,1)}), bf16[2,96,3072]{2,1,0:T(8,128)(2,1)S(1)}, u32[]{:S(2)}, u32[]{:S(2)}) async-start(bf16[2,96,3072]{2,1,0:T(8,128)(2,1)} %bitcast.39), calls=%async_computation.2 | async-start | bytes 2359296 | tf_op jit(solution)/shard_map/all_to_all | solution.py:38
  301.1 7.8 %all-to-all-start.3 = ((bf16[2,96,3072]{2,1,0:T(8,128)(2,1)}), bf16[2,96,3072]{2,1,0:T(8,128)(2,1)S(1)}, u32[]{:S(2)}, u32[]{:S(2)}) async-start(bf16[2,96,3072]{2,1,0:T(8,128)(2,1)} %bitcast.37), calls=%async_computation.3 | async-start | bytes 2359296 | tf_op jit(solution)/shard_map/all_to_all | solution.py:38
  307.2 1.8 copy-start
  308.8 1.1 copy-start.3
Sparse Core Ops, SparseCore 0:
  9.8 104.4 all-gather.3
  123.7 84.4 all-gather.5
  210.7 84.4 all-gather.7
where the time goes:
time: 320 us; the launch traced here: 319 us
  waiting for transfers between devices  199 us (62%)
  blocking collectives  60.9 us (19%)
  matrix products  18.8 us (6%)
  starting transfers between devices  16 us (5%)
  between operations  13.2 us (4%)
  local copies, waits for them, and re-layouts  6.48 us (2%)
  other arithmetic  4.08 us (1%)
    all_gather x2, waiting for transfers between devices, shards(): lax.all_gather(half_local, ROW, axis=0, tiled=True)  121 us
    all_gather x1, waiting for transfers between devices, shards(): all_orbitals = lax.all_gather(orbitals, ROW, axis=0, tiled=True)  73.8 us
    psum x3, blocking collectives, by_axis(): return functools.reduce(lax.psum, axes, value)  36.1 us
    all_to_all x1, blocking collectives, copy_for_each(): lax.all_to_all(jnp.broadcast_to(value[None], (size, *value.shape)), axis,...  24.7 us
    all_to_all x2, starting transfers between devices, sum_at_owner(): lax.all_to_all(tiles, axis, split_axis=0, concat_axis=0, tiled=True)  12 us
    dot_general x2, matrix products, shards(): lax.dot_general(half_local, lax.all_gather(half_local, ROW, axis=0, tiled...  9.64 us
    dot_general x2, matrix products, shards(): jnp.dot(collect(factors[aux], 'col', 1), all_orbitals, preferred_element_...  9.15 us
  transfers between devices with their start and end apart: 6, of which 5 were waited for; matrix products, arithmetic and copies ran while one was open for 5% of the time, Pallas kernels for 0%

commit v1 on v0

--- a/solution.py
+++ b/solution.py
@@ -45,7 +45,8 @@
 
 def shards(factors, orbitals, field_term):
     aux_count = factors.shape[0]
-    all_orbitals = lax.all_gather(orbitals, ROW, axis=0, tiled=True)
+    sent = jnp.stack([orbitals] * lax.axis_size(ROW))
+    all_orbitals = jnp.concatenate(lax.all_to_all(sent, ROW, 0, 0), axis=0)
     orbit_wide = orbitals.astype(jnp.float32)
     exchange = None
     gammas = []

time: 320 us -> 474 us (1.48)
  waiting for transfers between devices: 199 us -> 316 us
  blocking collectives: 60.9 us -> 92.4 us
    all_to_all x1, waiting for transfers between devices: 1.74 us -> 171 us  [shards(): all_orbitals = jnp.concatenate(lax.all_to_all(sent, ROW, 0, 0), axis=0)]
    all_gather x1 -> x0, waiting for transfers between devices: 73.8 us -> none  [shards(): all_orbitals = lax.all_gather(orbitals, ROW, axis=0, tiled=True)]
    psum x3, blocking collectives: 36.1 us -> 62.9 us  [by_axis(): return functools.reduce(lax.psum, axes, value)]
    all_gather x2, waiting for transfers between devices: 121 us -> 142 us  [shards(): lax.all_gather(half_local, ROW, axis=0, tiled=True)]
    all_to_all x1 -> x2, blocking collectives: 24.7 us -> 29.6 us  [copy_for_each(): lax.all_to_all(jnp.broadcast_to(value[None], (size, *value.shape)), axis,...]
  transfers between devices with their start and end apart: 6 -> 5, of which waited for: 5 -> 4; matrix products, arithmetic and copies ran while one was open for 5% -> 3% of each run, Pallas kernels for 0% -> 0%
where the time goes in v1:
time: 474 us; the launch traced here: 473 us
  waiting for transfers between devices  316 us (67%)
  blocking collectives  92.4 us (19%)
  starting transfers between devices  19.5 us (4%)
  matrix products  18.8 us (4%)
  between operations  13.6 us (3%)
  local copies, waits for them, and re-layouts  8.85 us (2%)
    all_to_all x1, waiting for transfers between devices, shards(): all_orbitals = jnp.concatenate(lax.all_to_all(sent, ROW, 0, 0), axis=0)  171 us
    all_gather x2, waiting for transfers between devices, shards(): lax.all_gather(half_local, ROW, axis=0, tiled=True)  142 us
    psum x3, blocking collectives, by_axis(): return functools.reduce(lax.psum, axes, value)  62.9 us
    all_to_all x2, blocking collectives, copy_for_each(): lax.all_to_all(jnp.broadcast_to(value[None], (size, *value.shape)), axis,...  29.6 us
    all_to_all x2, starting transfers between devices, sum_at_owner(): lax.all_to_all(tiles, axis, split_axis=0, concat_axis=0, tiled=True)  12 us
    dot_general x2, matrix products, shards(): lax.dot_general(half_local, lax.all_gather(half_local, ROW, axis=0, tiled...  9.64 us
  transfers between devices with their start and end apart: 5, of which 4 were waited for; matrix products, arithmetic and copies ran while one was open for 3% of the time, Pallas kernels for 0%

profile of v1, /device:TPU:513, one launch (start us, length us, event | category | flops | bytes accessed | tf_op | source)
XLA Modules:
  0.0 473.1 jit_solution(11344253183871000055)
XLA Ops:
  6.5 1.3 slice_bitcast_fusion
  7.9 0.1 broadcast_in_dim.17
  8.0 24.7 %all_to_all.25 = bf16[2,96,3072]{2,1,0:T(8,128)(2,1)S(1)} all-to-all(bf16[2,96,3072]{2,1,0:T(8,128)(2,1)S(1)} %broadcast_in_dim.17), channel_id=1, replica_groups=mesh['grp'=2,'row_0'=8,'row_1'=8,'col'=2] {'col'}, dimensions={0} | all-to-all | bytes 2359296 | tf_op jit(solution)/shard_map/all_to_all | solution.py:15
  32.7 0.1 broadcast_in_dim.15
  32.9 4.8 %all_to_all.26 = bf16[2,96,3072]{2,1,0:T(8,128)(2,1)S(1)} all-to-all(bf16[2,96,3072]{2,1,0:T(8,128)(2,1)S(1)} %broadcast_in_dim.15), channel_id=1, replica_groups=mesh['grp'=2,'row_0'=8,'row_1'=8,'col'=2] {'col'}, dimensions={0} | all-to-all | bytes 2359296 | tf_op jit(solution)/shard_map/all_to_all | solution.py:15
  37.7 3.4 stack.8
  41.1 7.4 %all-to-all-start.1 = ((bf16[64,96,512]{2,1,0:T(8,128)(2,1)}), bf16[64,96,512]{2,1,0:T(8,128)(2,1)}, u32[]{:S(2)}, u32[]{:S(2)}) async-start(bf16[64,96,512]{2,1,0:T(8,128)(2,1)} %stack.8), calls=%async_computation.1 | async-start | bytes 12582912 | tf_op jit(solution)/shard_map/all_to_all | solution.py:49
  48.6 0.1 copy.11
  48.7 0.1 copy.10
  48.8 170.7 %all-to-all-done.1 = bf16[64,96,512]{2,1,0:T(8,128)(2,1)} async-done(((bf16[64,96,512]{2,1,0:T(8,128)(2,1)}), bf16[64,96,512]{2,1,0:T(8,128)(2,1)}, u32[]{:S(2)}, u32[]{:S(2)}) %all-to-all-start.1) | async-done | bytes 6291488 | tf_op jit(solution)/shard_map/all_to_all | solution.py:49
  219.5 3.9 convolution_convert_fusion.2
  223.5 5.3 %fusion = (f32[]{:T(128)}, f32[]{:T(128)}, bf16[96,512]{1,0:T(8,128)(2,1)}) fusion(bf16[96,512]{1,0:T(8,128)(2,1)S(1)} %copy-done.5, bf16[96,512]{1,0:T(8,128)(2,1)S(1)} %convolution_convert_fusion.2, bf16[96,6144]{1,0:T(8,128)(2,1)S(1)} %bitcast.43, bf16[6144,512]{1,0:T(8,128)(2,1)} %bitcast.2), kind=kOutput, calls=%fused_computation.13 | convolution fusion | flops 604372992 | bytes 7766024 | tf_op jit(solution)/shard_map/dot_general | solution.py:54
  228.8 0.1 all-gather.5.cloned.1.call-start
  228.9 0.7 all-gather.5.cloned.1.call-update
  229.6 1.4 pad_maximum_fusion
  231.0 36.2 %psum.21 = f32[2]{0:T(128)S(1)} all-reduce(f32[2]{0:T(128)S(1)} %pad_maximum_fusion), channel_id=1, replica_groups=mesh['grp'=2,'row_0'=8,'row_1'=8,'col'=2] {'row_0'}, use_global_device_ids=true, to_apply=%region_2.0 | all-reduce | flops 2 | bytes 16 | tf_op jit(solution)/shard_map/psum | solution.py:43
  267.3 16.8 %psum.22 = f32[2]{0:T(128)S(1)} all-reduce(f32[2]{0:T(128)S(1)} %psum.21), channel_id=1, replica_groups=mesh['grp'=2,'row_0'=8,'row_1'=8,'col'=2] {'row_1'}, use_global_device_ids=true, to_apply=%region_3.0 | all-reduce | flops 2 | bytes 16 | tf_op jit(solution)/shard_map/psum | solution.py:43
  284.0 9.9 %psum.23 = f32[2]{0:T(128)S(1)} all-reduce(f32[2]{0:T(128)S(1)} %psum.22), channel_id=1, replica_groups=mesh['grp'=2,'row_0'=8,'row_1'=8,'col'=2] {'col'}, use_global_device_ids=true, to_apply=%region_4.0 | all-reduce | flops 2 | bytes 16 | tf_op jit(solution)/shard_map/psum | solution.py:43
  293.9 0.6 fusion.2
  294.5 67.5 %all-gather.3.cloned.1.call-done = bf16[6144,512]{1,0:T(8,128)(2,1)} async-done(((bf16[96,512]{1,0:T(8,128)(2,1)}), bf16[6144,512]{1,0:T(8,128)(2,1)}) %all-gather.3.cloned.1.call-update) | async-done | bytes 6291472 | tf_op jit(solution)/shard_map/all_gather | solution.py:61
  362.0 4.9 %convolution_convert_fusion.1 = bf16[96,6144]{1,0:T(8,128)(2,1)S(1)} fusion(bf16[96,512]{1,0:T(8,128)(2,1)} %get-tuple-element.11, bf16[6144,512]{1,0:T(8,128)(2,1)} %all-gather.3.cloned.1.call-done), kind=kOutput, calls=%fused_computation.1 | convolution fusion | flops 604569600 | bytes 7569408 | tf_op jit(solution)/shard_map/dot_general | solution.py:59
  366.8 1.1 copy.15
  367.9 6.1 %all-to-all-start.3 = ((bf16[2,96,3072]{2,1,0:T(8,128)(2,1)}), bf16[2,96,3072]{2,1,0:T(8,128)(2,1)S(1)}, u32[]{:S(2)}, u32[]{:S(2)}) async-start(bf16[2,96,3072]{2,1,0:T(8,128)(2,1)} %bitcast.40), calls=%async_computation.3 | async-start | bytes 2359296 | tf_op jit(solution)/shard_map/all_to_all | solution.py:38
  374.0 74.9 %all-gather.5.cloned.1.call-done = bf16[6144,512]{1,0:T(8,128)(2,1)} async-done(((bf16[96,512]{1,0:T(8,128)(2,1)}), bf16[6144,512]{1,0:T(8,128)(2,1)}) %all-gather.5.cloned.1.call-update) | async-done | bytes 6291472 | tf_op jit(solution)/shard_map/all_gather | solution.py:61
  448.9 4.8 %convolution_convert_fusion = bf16[96,6144]{1,0:T(8,128)(2,1)S(1)} fusion(bf16[96,512]{1,0:T(8,128)(2,1)S(1)} %copy-done.2, bf16[6144,512]{1,0:T(8,128)(2,1)} %all-gather.5.cloned.1.call-done), kind=kOutput, calls=%fused_computation | convolution fusion | flops 604569600 | bytes 7569408 | tf_op jit(solution)/shard_map/dot_general | solution.py:59
  453.7 1.1 copy.14
  454.8 5.9 %all-to-all-start.4 = ((bf16[2,96,3072]{2,1,0:T(8,128)(2,1)}), bf16[2,96,3072]{2,1,0:T(8,128)(2,1)S(1)}, u32[]{:S(2)}, u32[]{:S(2)}) async-start(bf16[2,96,3072]{2,1,0:T(8,128)(2,1)} %bitcast.38), calls=%async_computation.4 | async-start | bytes 2359296 | tf_op jit(solution)/shard_map/all_to_all | solution.py:38
  460.7 0.2 convert_reduce_fusion.1
  461.0 1.6 all-to-all-done.4
  462.6 0.2 convert_reduce_fusion
  462.8 0.8 copy-done.3
  463.6 2.6 subtract_convert_fusion
  (14 shorter events, 0.1 us)
Async XLA Ops:
  32.9 4.8 %copy-start.4 = (bf16[96,512]{1,0:T(8,128)(2,1)S(1)}, bf16[96,512]{1,0:T(8,128)(2,1)}, u32[]{:S(2)}) copy-start(bf16[96,512]{1,0:T(8,128)(2,1)} %param.4) | copy-start | bytes 294916
  41.1 178.4 %all-to-all-start.1 = ((bf16[64,96,512]{2,1,0:T(8,128)(2,1)}), bf16[64,96,512]{2,1,0:T(8,128)(2,1)}, u32[]{:S(2)}, u32[]{:S(2)}) async-start(bf16[64,96,512]{2,1,0:T(8,128)(2,1)} %stack.8), calls=%async_computation.1 | async-start | bytes 12582912 | tf_op jit(solution)/shard_map/all_to_all | solution.py:49
  48.5 313.5 %all-gather.3.cloned.1.call-start = ((), (), s32[]{:S(2)}) async-start(), calls=%async_computation.5 | async-start | bytes 6389760 | tf_op jit(solution)/shard_map/all_gather | solution.py:61
  219.5 4.0 copy-start.5
  223.5 5.3 %copy-start.1 = (bf16[96,512]{1,0:T(8,128)(2,1)}, bf16[96,512]{1,0:T(8,128)(2,1)S(1)}, u32[]{:S(2)}) copy-start(bf16[96,512]{1,0:T(8,128)(2,1)S(1)} %convolution_convert_fusion.2) | copy-start | bytes 294916
  228.8 220.1 %all-gather.5.cloned.1.call-start = ((), (), s32[]{:S(2)}) async-start(), calls=%async_computation.6 | async-start | bytes 6389760 | tf_op jit(solution)/shard_map/all_gather | solution.py:61
  367.9 81.0 %copy-start.2 = (bf16[96,512]{1,0:T(8,128)(2,1)S(1)}, bf16[96,512]{1,0:T(8,128)(2,1)}, u32[]{:S(2)}) copy-start(bf16[96,512]{1,0:T(8,128)(2,1)} %copy-done.1) | copy-start | bytes 294916
  367.9 86.9 %all-to-all-start.3 = ((bf16[2,96,3072]{2,1,0:T(8,128)(2,1)}), bf16[2,96,3072]{2,1,0:T(8,128)(2,1)S(1)}, u32[]{:S(2)}, u32[]{:S(2)}) async-start(bf16[2,96,3072]{2,1,0:T(8,128)(2,1)} %bitcast.40), calls=%async_computation.3 | async-start | bytes 2359296 | tf_op jit(solution)/shard_map/all_to_all | solution.py:38
  454.8 7.8 %all-to-all-start.4 = ((bf16[2,96,3072]{2,1,0:T(8,128)(2,1)}), bf16[2,96,3072]{2,1,0:T(8,128)(2,1)S(1)}, u32[]{:S(2)}, u32[]{:S(2)}) async-start(bf16[2,96,3072]{2,1,0:T(8,128)(2,1)} %bitcast.38), calls=%async_computation.4 | async-start | bytes 2359296 | tf_op jit(solution)/shard_map/all_to_all | solution.py:38
  460.9 1.8 copy-start
  462.6 1.1 copy-start.3
Sparse Core Ops, SparseCore 0:
  228.9 132.9 all-gather.2
  364.4 84.4 all-gather.4
